TPU v7x, 8 devices: a whole 2x2x1 slice. The times are simulated.
8 devices in a mesh: dp: 1 (over z), ey: 2 (over y), ex: 4 (over x, core).
Axes of the slice: x: 2, y: 2, z: 1, core: 2. Of those that a mesh axis runs over, the one named last changes fastest.
Arguments:
- x: bfloat16 [1024, 2048], P(('dp', 'ey', 'ex'))
- ids: int32 [1024, 6], P(('dp', 'ey', 'ex'))
- gates: float32 [1024, 6], P(('dp', 'ey', 'ex'))
- w1: bfloat16 [64, 2048, 1408], P(('ey', 'ex'))
- w3: bfloat16 [64, 2048, 1408], P(('ey', 'ex'))
- w2: bfloat16 [64, 1408, 2048], P(('ey', 'ex'))
Outputs:
- output: bfloat16 [1024, 2048], P(('dp', 'ey', 'ex'))
All inputs are finite; a program needn't handle non-finite values.
Results may differ from a plain program's by a relative error of at most 0.00637368.
Values are sent between devices in bfloat16 or wider.
A program may use at most 1 GiB of HBM per device.

v0:
```python
import jax
import jax.numpy as jnp
from jax import lax
from jax.sharding import PartitionSpec as P

CAPF = 2


def solution(mesh):
    nx = mesh.shape["ex"]
    nd = mesh.shape["ey"] * nx
    axes = ("ey", "ex")
    tok = P(("dp", "ey", "ex"), None)
    wsp = P(("ey", "ex"), None, None)

    def local(x, ids, gates, w1, w3, w2):
        t, hd = x.shape
        top = ids.shape[1]
        el = w1.shape[0]
        cap = min(t, CAPF * t * top // nd)
        me = lax.axis_index("ey") * nx + lax.axis_index("ex")
        dev = ids // el
        hit = jnp.any(dev[:, :, None] == jnp.arange(nd)[None, None, :], axis=1)
        rank = jnp.cumsum(hit.astype(jnp.int32), axis=0) - 1
        kept = hit & (rank < cap)
        slot = jnp.where(kept, rank, cap)
        dst = jnp.broadcast_to(jnp.arange(nd)[None, :], (t, nd))
        src = jnp.broadcast_to(jnp.arange(t)[:, None], (t, nd))
        sx = jnp.zeros((nd, cap, hd), x.dtype).at[dst, slot].set(x[src], mode="drop")
        si = jnp.full((nd, cap, top), -1, jnp.int32).at[dst, slot].set(ids[src], mode="drop")
        sg = jnp.zeros((nd, cap, top), jnp.float32).at[dst, slot].set(gates[src], mode="drop")
        rx = lax.all_to_all(sx, axes, 0, 0, tiled=True).reshape(nd * cap, hd)
        ri = lax.all_to_all(si, axes, 0, 0, tiled=True).reshape(nd * cap, top)
        rg = lax.all_to_all(sg, axes, 0, 0, tiled=True).reshape(nd * cap, top)
        a1 = jnp.einsum("rh,ehf->erf", rx, w1, preferred_element_type=jnp.float32)
        a3 = jnp.einsum("rh,ehf->erf", rx, w3, preferred_element_type=jnp.float32)
        hh = (jax.nn.silu(a1) * a3).astype(jnp.bfloat16)
        o = jnp.einsum("erf,efh->erh", hh, w2, preferred_element_type=jnp.float32).astype(jnp.bfloat16)
        eid = me * el + jnp.arange(el)
        coef = jnp.sum(jnp.where(ri[None, :, :] == eid[:, None, None], rg[None, :, :], 0.0), axis=2)
        part = jnp.sum(coef[:, :, None] * o, axis=0).reshape(nd, cap, hd)
        back = lax.all_to_all(part, axes, 0, 0, tiled=True)
        got = back[dst, jnp.minimum(slot, cap - 1)]
        moe_out = jnp.sum(jnp.where(kept[:, :, None], got, 0.0), axis=1)
        return (x.astype(jnp.float32) + moe_out).astype(jnp.bfloat16)

    return jax.shard_map(local, mesh=mesh, in_specs=(tok, tok, tok, wsp, wsp, wsp),
                         out_specs=tok, check_vma=False)
```

profile of v0, /device:TPU:0, one launch (start us, length us, event | category | flops | bytes accessed | tf_op | source)
XLA Modules:
  0.0 420.2 jit_solution(4231189203803234428)
XLA Ops:
  0.0 0.7 add_select_fusion
  0.7 0.8 copy.51
  1.5 0.0 copy-start.5
  1.5 0.1 copy.47
  1.6 0.2 reduce_window_sum.11
  1.8 0.0 copy-start.1
  1.8 0.6 fusion.18
  2.5 0.7 multiply_reduce_fusion.1
  3.2 0.7 and_reduce_fusion
  3.9 0.0 copy-done.1
  3.9 0.1 copy.50
  4.0 0.1 reshape.135
  4.2 0.1 reshape.107
  4.2 0.0 copy-done.5
  4.3 6.8 %scatter_custom_fusion = s32[6,1024]{0,1:T(8,128)S(1)} fusion(s32[1024]{0:T(1024)S(1)} %reshape.135, s32[128,6]{1,0:T(8,128)S(1)} %copy.51, s32[1024]{0:T(1024)S(1)} %broadcast_clamp_fusion, s32[]{:T(128)} %constant.41.clone.1), kind=kCustom, calls=%fused_computation.23 | custom fusion | bytes 24580
  11.0 0.8 copy.52
  11.8 4.3 %all-to-all-start = ((s32[8,128,6]{1,2,0:T(8,128)}), s32[8,128,6]{1,2,0:T(8,128)S(1)}, u32[]{:S(2)}, u32[]{:S(2)}) async-start(s32[8,128,6]{1,2,0:T(8,128)} %bitcast.3), calls=%async_computation | async-start | bytes 65536 | tf_op jit(solution)/shard_map/all_to_all | solution.py:33
  16.1 0.8 copy.53
  16.9 6.8 %scatter_custom_fusion.1 = f32[6,1024]{0,1:T(8,128)S(1)} fusion(s32[1024]{0:T(1024)S(1)} %reshape.135, f32[128,6]{1,0:T(8,128)S(1)} %copy.53, s32[1024]{0:T(1024)S(1)} %broadcast_clamp_fusion, f32[]{:T(128)} %constant.49.clone.1), kind=kCustom, calls=%fused_computation.21 | custom fusion | bytes 24580
  23.7 0.8 copy.54
  24.5 0.0 all-to-all-done
  24.5 2.9 all-to-all-start.1
  27.4 23.2 %scatter_custom_fusion.2 = bf16[1024,2048]{1,0:T(8,128)(2,1)} fusion(s32[1024]{0:T(1024)S(1)} %reshape.135, bf16[128,2048]{1,0:T(8,128)(2,1)} %param.6, s32[1024]{0:T(1024)S(1)} %broadcast_clamp_fusion, bf16[]{:T(256)} %constant.50.clone.1), kind=kCustom, calls=%fused_computation.17 | custom fusion | bytes 4194816
  50.6 0.0 all-to-all-done.1
  50.6 3.5 all-to-all-start.2
  54.1 0.7 select_reduce_fusion
  54.8 48.3 %all-to-all-done.2 = bf16[8,128,2048]{2,1,0:T(8,128)(2,1)} async-done(((bf16[8,128,2048]{2,1,0:T(8,128)(2,1)}), bf16[8,128,2048]{2,1,0:T(8,128)(2,1)}, u32[]{:S(2)}, u32[]{:S(2)}) %all-to-all-start.2) | async-done | bytes 4194336 | tf_op jit(solution)/shard_map/all_to_all | solution.py:32
  103.1 55.3 %fusion.22 = f32[1024,8,1408]{2,0,1:T(8,128)} fusion(bf16[1024,2048,1]{1,0,2:T(8,128)(2,1)} %bitcast.10, bf16[8,2048,1408]{2,1,0:T(8,128)(2,1)} %param.10), kind=kOutput, calls=%fused_computation.53 | convolution fusion | flops 47244640256 | bytes 96468992 | tf_op jit(solution)/shard_map/rh,ehf->erf/dot_general | solution.py:36
  158.4 0.0 copy-start.3
  158.4 63.5 %fusion.clone.4 = bf16[8,1024,1408]{2,1,0:T(8,128)(2,1)} fusion(f32[1024,8,1408]{2,0,1:T(8,128)} %fusion.22, bf16[1024,2048,1]{1,0,2:T(8,128)(2,1)} %bitcast.10, bf16[8,2048,1408]{2,1,0:T(8,128)(2,1)} %param.9), kind=kOutput, calls=%fused_computation.9.clone.clone.clone.1 | convolution fusion | flops 47313846272 | bytes 119537664 | tf_op jit(solution)/shard_map/rh,ehf->erf/dot_general | solution.py:35
  221.9 0.0 copy-done.3
  221.9 0.0 copy-start.4
  221.9 0.0 copy-start.2
  221.9 0.0 copy-start.6
  221.9 63.1 %multiply_reduce_fusion = f32[1024,2048]{1,0:T(8,128)} fusion(f32[8,1024]{1,0:T(8,128)S(1)} %copy-done.3, bf16[8,1408,2048]{2,1,0:T(8,128)(2,1)} %param.11, bf16[8,1024,1408]{2,1,0:T(8,128)(2,1)} %fusion.clone.4), kind=kOutput, calls=%fused_computation.7 | convolution fusion | flops 47309651968 | bytes 77627392 | tf_op jit(solution)/shard_map/erf,efh->erh/dot_general | solution.py:38
  285.0 4.0 all-to-all-start.3
  288.9 0.0 copy-done.4
  288.9 0.1 copy.55
  289.0 0.1 reshape.129
  289.1 0.0 copy-done.2
  289.1 0.0 copy-done.6
  289.2 0.1 copy.49
  289.3 0.0 copy-start
  289.3 93.3 %all-to-all-done.3 = f32[8,128,2048]{2,1,0:T(8,128)} async-done(((f32[8,128,2048]{2,1,0:T(8,128)}), f32[8,128,2048]{2,1,0:T(8,128)}, u32[]{:S(2)}, u32[]{:S(2)}) %all-to-all-start.3) | async-done | bytes 8388640 | tf_op jit(solution)/shard_map/all_to_all | solution.py:42
  382.7 29.7 %gather_fusion = f32[1024,2048]{1,0:T(8,128)} fusion(f32[8,128,2048]{2,1,0:T(8,128)} %all-to-all-done.3, s32[1024]{0:T(1024)S(1)} %reshape.129), kind=kCustom, calls=%fused_computation.3 | custom fusion | bytes 16785408 | tf_op jit(solution)/shard_map/gather | solution.py:43
  412.4 6.9 %fusion.4 = f32[128,2048]{1,0:T(8,128)S(1)} fusion(f32[1024,2048]{1,0:T(8,128)} %gather_fusion, pred[128,8]{1,0:T(8,128)(4,1)S(1)} %copy.49), kind=kLoop, calls=%fused_computation.16 | loop fusion | flops 3932160 | bytes 9438208 | tf_op jit(solution)/shard_map/reduce_sum | solution.py:44
  419.2 0.0 copy-done
  419.2 0.9 add_convert_fusion
  (9 shorter events, 0.1 us)
Async XLA Ops:
  1.5 2.7 copy-start.5
  1.8 2.1 copy-start.1
  11.8 12.7 %all-to-all-start = ((s32[8,128,6]{1,2,0:T(8,128)}), s32[8,128,6]{1,2,0:T(8,128)S(1)}, u32[]{:S(2)}, u32[]{:S(2)}) async-start(s32[8,128,6]{1,2,0:T(8,128)} %bitcast.3), calls=%async_computation | async-start | bytes 65536 | tf_op jit(solution)/shard_map/all_to_all | solution.py:33
  24.5 26.1 %all-to-all-start.1 = ((f32[8,128,6]{1,2,0:T(8,128)}), f32[8,128,6]{1,2,0:T(8,128)S(1)}, u32[]{:S(2)}, u32[]{:S(2)}) async-start(f32[8,128,6]{1,2,0:T(8,128)} %bitcast.6), calls=%async_computation.1 | async-start | bytes 65536 | tf_op jit(solution)/shard_map/all_to_all | solution.py:34
  50.6 52.5 %all-to-all-start.2 = ((bf16[8,128,2048]{2,1,0:T(8,128)(2,1)}), bf16[8,128,2048]{2,1,0:T(8,128)(2,1)}, u32[]{:S(2)}, u32[]{:S(2)}) async-start(bf16[8,128,2048]{2,1,0:T(8,128)(2,1)} %bitcast.74), calls=%async_computation.2 | async-start | bytes 8388608 | tf_op jit(solution)/shard_map/all_to_all | solution.py:32
  158.4 63.5 %copy-start.3 = (f32[8,1024]{1,0:T(8,128)S(1)}, f32[8,1024]{1,0:T(8,128)}, u32[]{:S(2)}) copy-start(f32[8,1024]{1,0:T(8,128)} %select_reduce_fusion) | copy-start | bytes 98308
  221.9 67.1 %copy-start.4 = (s32[128,8,1]{0,1,2:T(8,128)S(1)}, s32[128,8,1]{0,1,2:T(8,128)}, u32[]{:S(2)}) copy-start(s32[128,8,1]{0,1,2:T(8,128)} %get-tuple-element.5) | copy-start | bytes 12292
  221.9 67.3 %copy-start.2 = (s32[128,8]{0,1:T(8,128)S(1)}, s32[128,8]{0,1:T(8,128)}, u32[]{:S(2)}) copy-start(s32[128,8]{0,1:T(8,128)} %copy-done.1) | copy-start | bytes 12292
  221.9 67.3 %copy-start.6 = (pred[128,8]{0,1:T(8,128)(4,1)S(1)}, pred[128,8]{0,1:T(8,128)(4,1)}, u32[]{:S(2)}) copy-start(pred[128,8]{0,1:T(8,128)(4,1)} %copy-done.5) | copy-start | bytes 3076
  285.0 97.7 %all-to-all-start.3 = ((f32[8,128,2048]{2,1,0:T(8,128)}), f32[8,128,2048]{2,1,0:T(8,128)}, u32[]{:S(2)}, u32[]{:S(2)}) async-start(f32[8,128,2048]{2,1,0:T(8,128)} %bitcast.75), calls=%async_computation.3 | async-start | bytes 16777216 | tf_op jit(solution)/shard_map/all_to_all | solution.py:42
  289.3 129.9 %copy-start = (bf16[128,2048]{1,0:T(8,128)(2,1)S(1)}, bf16[128,2048]{1,0:T(8,128)(2,1)}, u32[]{:S(2)}) copy-start(bf16[128,2048]{1,0:T(8,128)(2,1)} %param.6) | copy-start | bytes 1572868
where the time goes:
time: 421 us; the launch traced here: 420 us
  matrix products  182 us (43%)
  waiting for transfers between devices  142 us (34%)
  local copies, waits for them, and re-layouts  70.4 us (17%)
  starting transfers between devices  14.7 us (3%)
  other arithmetic  11.5 us (3%)
    all_to_all x1, waiting for transfers between devices, local(): back = lax.all_to_all(part, axes, 0, 0, tiled=True)  93.3 us
    dot_general x1, matrix products, local(): a1 = jnp.einsum('rh,ehf->erf', rx, w1, preferred_element_type=jnp.float32)  63.5 us
    dot_general x1, matrix products, local(): jnp.einsum('erf,efh->erh', hh, w2, preferred_element_type=jnp.float32)  63.1 us
    dot_general x1, matrix products, local(): a3 = jnp.einsum('rh,ehf->erf', rx, w3, preferred_element_type=jnp.float32)  55.3 us
    all_to_all x1, waiting for transfers between devices, local(): rx = lax.all_to_all(sx, axes, 0, 0, tiled=True).reshape(nd * cap, hd)  48.3 us
    unnamed x23, local copies, waits for them, and re-layouts  40.1 us
    gather x1, local copies, waits for them, and re-layouts, local(): got = back[dst, jnp.minimum(slot, cap - 1)]  29.7 us
  transfers between devices with their start and end apart: 4, of which 2 were waited for; matrix products, arithmetic and copies ran while one was open for 8% of the time, Pallas kernels for 0%

commit v1 on v0

v1 whole, which is shorter than its diff:
```python
import functools

import jax
import jax.numpy as jnp
from jax import lax
from jax.experimental import pallas as pl
from jax.experimental.pallas import tpu as pltpu
from jax.sharding import PartitionSpec as P

CAPF = 2
MESH = pl.DeviceIdType.MESH
ANY = pl.BlockSpec(memory_space=pl.ANY)
VM = pl.BlockSpec(memory_space=pltpu.VMEM)
SM = pl.BlockSpec(memory_space=pltpu.SMEM)
VLIM = 67043328


def place():
    dp, ey, ex = lax.axis_index("dp"), lax.axis_index("ey"), lax.axis_index("ex")
    ix, ic = ex // 2, ex % 2
    part = (dp, ey, ix * 2 + (1 - ic))
    xn = (dp, ey, (1 - ix) * 2 + ic)
    yn = (dp, 1 - ey, ex)
    return dp, ey, ix, ic, part, xn, yn


def gather_kernel(cap, x_ref, ids_ref, gates_ref, xall_ref, pos_ref, tok_ref, cum_ref,
                  meta, ssem, rsem, msend, mrecv):
    t, hd = x_ref.shape
    top = ids_ref.shape[1]
    hf = t // 2
    dp, ey, ix, ic, part, xn, yn = place()
    me = ey * 4 + ix * 2 + ic
    dxn = ey * 4 + (1 - ix) * 2 + ic
    dyn = (1 - ey) * 4 + ix * 2 + ic
    ddg = (1 - ey) * 4 + (1 - ix) * 2 + ic

    def dev(d):
        return (dp, d // 4, d % 4)

    pad = jnp.zeros((t, 8 - top), jnp.float32)
    both = jnp.concatenate([ids_ref[...].astype(jnp.float32), pad - 1.0,
                            gates_ref[...], pad, jnp.zeros((t, 112), jnp.float32)], axis=1)
    meta[me] = jnp.transpose(both)[:16]

    barrier = pltpu.get_barrier_semaphore()
    for j in range(1, 8):
        pl.semaphore_signal(barrier, inc=1, device_id=dev((me + j) % 8), device_id_type=MESH)
    pl.semaphore_wait(barrier, 7)

    mcopies = []
    for j in range(1, 8):
        c = pltpu.make_async_remote_copy(
            src_ref=meta.at[me], dst_ref=meta.at[me], send_sem=msend.at[j - 1],
            recv_sem=mrecv.at[j - 1], device_id=dev((me + j) % 8), device_id_type=MESH)
        c.start()
        mcopies.append(c)

    def rows(d, h):
        return pl.ds(pl.multiple_of(d * t + h * hf, hf), hf)

    def rc(k, src, d, h, to):
        return pltpu.make_async_remote_copy(
            src_ref=src, dst_ref=xall_ref.at[rows(d, h)], send_sem=ssem.at[k],
            recv_sem=rsem.at[k], device_id=to, device_id_type=MESH)

    def own(k, h, to):
        return rc(k, x_ref.at[pl.ds(h * hf, hf)], me, h, to)

    def fwd(k, d, h, to):
        return rc(k, xall_ref.at[rows(d, h)], d, h, to)

    cs = {0: own(0, 0, xn), 1: own(1, 1, xn), 2: own(2, 1, yn), 3: own(3, 0, yn),
          4: own(4, 0, part), 5: own(5, 1, part),
          6: fwd(6, dxn, 0, yn), 7: fwd(7, dyn, 1, xn),
          8: fwd(8, dxn, 0, part), 9: fwd(9, dxn, 1, part),
          10: fwd(10, dyn, 1, part), 11: fwd(11, dyn, 0, part),
          12: fwd(12, ddg, 0, part), 13: fwd(13, ddg, 1, part)}
    for k in (0, 2, 1, 3, 4, 5):
        cs[k].start()
    xall_ref[pl.ds(pl.multiple_of(me * t, t), t)] = x_ref[...]

    for c in mcopies:
        c.wait_recv()

    el = pos_ref.shape[0]
    ri = lax.broadcasted_iota(jnp.int32, (128, 128), 0)
    ci = lax.broadcasted_iota(jnp.int32, (128, 128), 1)
    upper = (ri < ci).astype(jnp.bfloat16)
    sub = lax.broadcasted_iota(jnp.int32, (el, t), 0)
    lane = lax.broadcasted_iota(jnp.int32, (el, 128), 1)
    base = jnp.zeros((el, 1), jnp.float32)
    cum = jnp.zeros((el, 128), jnp.float32)
    first = (me * el).astype(jnp.float32)
    for b in range(8):
        m = meta[b]
        idb, gb = m[:8], m[8:]
        mask = jnp.zeros((el, t), jnp.float32)
        coef = jnp.zeros((el, t), jnp.float32)
        for e in range(el):
            eq = idb == first + e
            mask = jnp.where(sub == e, jnp.max(jnp.where(eq, 1.0, 0.0), axis=0, keepdims=True), mask)
            coef = jnp.where(sub == e, jnp.sum(jnp.where(eq, gb, 0.0), axis=0, keepdims=True), coef)
        hit = jnp.broadcast_to(jnp.max(mask, axis=0, keepdims=True), (el, t))
        rank = jnp.dot(hit.astype(jnp.bfloat16), upper, preferred_element_type=jnp.float32)
        mask = jnp.where(rank < cap, mask, 0.0)
        within = jnp.dot(mask.astype(jnp.bfloat16), upper, preferred_element_type=jnp.float32)
        pos = jnp.where(mask > 0.0, within + base, -1.0)
        cum = jnp.where(lane == b, base, cum)
        base = base + jnp.sum(mask, axis=1, keepdims=True)
        pos_ref[:, b * t:(b + 1) * t] = pos
        tok_ref[b * t:(b + 1) * t, :] = jnp.transpose(
            jnp.concatenate([pos, coef, jnp.zeros((128 - 2 * el, t), jnp.float32)], axis=0))
    cum_ref[...] = jnp.where(lane == 8, base, cum).astype(jnp.int32)

    cs[0].wait_recv()
    cs[6].start()
    cs[8].start()
    cs[2].wait_recv()
    cs[7].start()
    cs[10].start()
    cs[1].wait_recv()
    cs[9].start()
    cs[3].wait_recv()
    cs[11].start()
    cs[6].wait_recv()
    cs[12].start()
    cs[7].wait_recv()
    cs[13].start()
    for k in (4, 5, 8, 9, 10, 11, 12, 13):
        cs[k].wait_recv()
    for k in range(14):
        cs[k].wait_send()
    for c in mcopies:
        c.wait_send()


def expert_kernel(cum_ref, pos_ref, tok_ref, x_ref, w1_ref, w3_ref, w2_ref, acc_ref,
                  w13b, w2b, xg, ob, order, sems):
    el, hd, f = w1_ref.shape
    n = x_ref.shape[0]
    tb = 256
    nb = n // tb
    per = tb // 128

    def listing(e, k):
        @pl.when(cum_ref[e, 8] > 0)
        def _():
            order[k] = e
        return jnp.where(cum_ref[e, 8] > 0, k + 1, k)

    nact = lax.fori_loop(0, el, listing, 0)

    def copies(k):
        e, s = order[k], k % 2
        return (pltpu.make_async_copy(w1_ref.at[e], w13b.at[s, :, pl.ds(0, f)], sems.at[s, 0]),
                pltpu.make_async_copy(w3_ref.at[e], w13b.at[s, :, pl.ds(f, f)], sems.at[s, 1]),
                pltpu.make_async_copy(w2_ref.at[e], w2b.at[s], sems.at[s, 2]))

    def start(k):
        @pl.when(k < nact)
        def _():
            for c in copies(k):
                c.start()

    start(0)
    start(1)
    acc_ref[...] = jnp.zeros_like(acc_ref)

    def tile(e, s, r0, tm):
        def overlap(b):
            return (cum_ref[e, b * per] < r0 + tm) & (cum_ref[e, (b + 1) * per] > r0)

        r0f = r0.astype(jnp.float32)
        xg[:tm] = jnp.zeros((tm, hd), xg.dtype)

        def pick(b, c):
            @pl.when(overlap(b))
            def _():
                toks = pl.ds(pl.multiple_of(b * tb, tb), tb)
                p = pos_ref[pl.ds(e, 1), toks]
                rows = lax.broadcasted_iota(jnp.int32, (tm, tb), 0).astype(jnp.float32) + r0f
                sel = jnp.where(rows == p, 1.0, 0.0).astype(jnp.bfloat16)
                xg[:tm] += jnp.dot(sel, x_ref[toks, :], preferred_element_type=jnp.float32).astype(xg.dtype)
            return c

        lax.fori_loop(0, nb, pick, 0)
        a = jnp.dot(xg[:tm], w13b[s], preferred_element_type=jnp.float32)
        a1, a3 = a[:, :f], a[:, f:]
        h = (jax.nn.silu(a1) * a3).astype(jnp.bfloat16)
        ob[:tm] = jnp.dot(h, w2b[s], preferred_element_type=jnp.float32).astype(jnp.bfloat16)

        def put(b, c):
            @pl.when(overlap(b))
            def _():
                toks = pl.ds(pl.multiple_of(b * tb, tb), tb)
                tk = tok_ref[toks, :]
                lane = lax.broadcasted_iota(jnp.int32, tk.shape, 1)
                p = jnp.sum(jnp.where(lane == e, tk, 0.0), axis=1, keepdims=True)
                g = jnp.sum(jnp.where(lane == el + e, tk, 0.0), axis=1, keepdims=True)
                rows = lax.broadcasted_iota(jnp.int32, (tb, tm), 1).astype(jnp.float32) + r0f
                sel = jnp.where(rows == p, 1.0, 0.0).astype(jnp.bfloat16)
                acc_ref[toks, :] += g * jnp.dot(sel, ob[:tm], preferred_element_type=jnp.float32)
            return c

        lax.fori_loop(0, nb, put, 0)

    def expert(k, c):
        e, s = order[k], k % 2
        for cp in copies(k):
            cp.wait()
        cnt = cum_ref[e, 8]
        rem = cnt % 256
        big = cnt // 256 + jnp.where(rem > 128, 1, 0)

        def step(i, c):
            tile(e, s, i * 256, 256)
            return c

        lax.fori_loop(0, big, step, 0)

        @pl.when((rem > 0) & (rem <= 128))
        def _():
            tile(e, s, big * 256, 128)

        start(k + 2)
        return c

    lax.fori_loop(0, nact, expert, 0)


def scatter_kernel(nc, part_ref, x_ref, y_ref, own, prt, rx, ry, r2, lsem, s0, q0, s1, q1, s2, q2):
    dp, ey, ix, ic, part, xn, yn = place()
    hd = x_ref.shape[1]
    half = hd // 2
    w = half // nc
    barrier = pltpu.get_barrier_semaphore()
    for d in (part, xn, yn):
        pl.semaphore_signal(barrier, inc=1, device_id=d, device_id_type=MESH)

    chunks = [(s, i) for i in range(nc) for s in range(2)]

    def cols(s, i):
        return pl.ds(s * half + i * w, w)

    loads, ph0, ph1, ph2 = {}, {}, {}, {}
    for s, i in chunks:
        k = i * 2 + s
        c = cols(s, i)
        loads[s, i] = pltpu.make_async_copy(part_ref.at[:, :, ic, :, c], own.at[:, :, :, c], lsem.at[k])
        ph0[s, i] = pltpu.make_async_remote_copy(
            src_ref=part_ref.at[:, :, 1 - ic, :, c], dst_ref=prt.at[:, :, :, c], send_sem=s0.at[k],
            recv_sem=q0.at[k], device_id=part, device_id_type=MESH)
        if s == 0:
            ph1[s, i] = pltpu.make_async_remote_copy(
                src_ref=own.at[:, 1 - ix, :, c], dst_ref=rx.at[:, :, pl.ds(i * w, w)], send_sem=s1.at[k],
                recv_sem=q1.at[k], device_id=xn, device_id_type=MESH)
            ph2[s, i] = pltpu.make_async_remote_copy(
                src_ref=own.at[1 - ey, ix, :, c], dst_ref=r2.at[:, c], send_sem=s2.at[k],
                recv_sem=q2.at[k], device_id=yn, device_id_type=MESH)
        else:
            ph1[s, i] = pltpu.make_async_remote_copy(
                src_ref=own.at[1 - ey, :, :, c], dst_ref=ry.at[:, :, pl.ds(i * w, w)], send_sem=s1.at[k],
                recv_sem=q1.at[k], device_id=yn, device_id_type=MESH)
            ph2[s, i] = pltpu.make_async_remote_copy(
                src_ref=own.at[ey, 1 - ix, :, c], dst_ref=r2.at[:, c], send_sem=s2.at[k],
                recv_sem=q2.at[k], device_id=xn, device_id_type=MESH)
    for k in chunks:
        loads[k].start()
    pl.semaphore_wait(barrier, 3)
    for k in chunks:
        ph0[k].start()
    for s, i in chunks:
        c = cols(s, i)
        loads[s, i].wait()
        ph0[s, i].wait_recv()
        if s == 0:
            own[:, 1 - ix, :, c] += prt[:, 1 - ix, :, c]
        else:
            own[1 - ey, :, :, c] += prt[1 - ey, :, :, c]
        ph1[s, i].start()
        if s == 0:
            own[:, ix, :, c] += prt[:, ix, :, c]
        else:
            own[ey, :, :, c] += prt[ey, :, :, c]
    for s, i in chunks:
        c = cols(s, i)
        ph1[s, i].wait_recv()
        if s == 0:
            own[1 - ey, ix, :, c] += rx[1 - ey, :, i * w:(i + 1) * w]
        else:
            own[ey, 1 - ix, :, c] += ry[1 - ix, :, i * w:(i + 1) * w]
        ph2[s, i].start()
        if s == 0:
            own[ey, ix, :, c] += rx[ey, :, i * w:(i + 1) * w]
        else:
            own[ey, ix, :, c] += ry[ix, :, i * w:(i + 1) * w]
    for s, i in chunks:
        c = cols(s, i)
        ph2[s, i].wait_recv()
        y_ref[:, c] = (x_ref[:, c].astype(jnp.float32) + (own[ey, ix, :, c] + r2[:, c])).astype(y_ref.dtype)
    for k in chunks:
        ph0[k].wait_send()
        ph1[k].wait_send()
        ph2[k].wait_send()


def solution(mesh):
    nx = mesh.shape["ex"]
    nd = mesh.shape["ey"] * nx
    tok = P(("dp", "ey", "ex"), None)
    wsp = P(("ey", "ex"), None, None)
    f32 = jnp.float32
    dma = pltpu.SemaphoreType.DMA

    def local(x, ids, gates, w1, w3, w2):
        t, hd = x.shape
        top = ids.shape[1]
        el, _, f = w1.shape
        n = nd * t
        cap = min(t, CAPF * t * top // nd)
        xall, pos, tokt, cum = pl.pallas_call(
            functools.partial(gather_kernel, cap),
            out_shape=(jax.ShapeDtypeStruct((n, hd), x.dtype), jax.ShapeDtypeStruct((el, n), f32),
                       jax.ShapeDtypeStruct((n, 128), f32), jax.ShapeDtypeStruct((el, 128), jnp.int32)),
            in_specs=[VM] * 3, out_specs=(VM,) * 4,
            scratch_shapes=[pltpu.VMEM((nd, 16, t), f32), dma((14,)), dma((14,)), dma((7,)), dma((7,))],
            compiler_params=pltpu.CompilerParams(collective_id=0, has_side_effects=True),
            name="gather")(x, ids, gates)
        acc = pl.pallas_call(
            expert_kernel,
            out_shape=jax.ShapeDtypeStruct((n, hd), f32),
            in_specs=[SM, VM, VM, VM, ANY, ANY, ANY], out_specs=VM,
            scratch_shapes=[pltpu.VMEM((2, hd, 2 * f), w1.dtype), pltpu.VMEM((2, f, hd), w2.dtype),
                            pltpu.VMEM((256, hd), x.dtype), pltpu.VMEM((256, hd), x.dtype),
                            pltpu.SMEM((el + 2,), jnp.int32), dma((2, 3))],
            compiler_params=pltpu.CompilerParams(vmem_limit_bytes=VLIM),
            name="experts")(cum, pos, tokt, xall, w1, w3, w2)
        nc = 4
        half = hd // 2
        y = pl.pallas_call(
            functools.partial(scatter_kernel, nc),
            out_shape=jax.ShapeDtypeStruct((t, hd), x.dtype),
            in_specs=[ANY, VM], out_specs=VM,
            scratch_shapes=[pltpu.VMEM((2, 2, t, hd), f32), pltpu.VMEM((2, 2, t, hd), f32),
                            pltpu.VMEM((2, t, half), f32), pltpu.VMEM((2, t, half), f32),
                            pltpu.VMEM((t, hd), f32)] + [dma((2 * nc,))] * 7,
            compiler_params=pltpu.CompilerParams(collective_id=1, has_side_effects=True),
            name="scatter")(acc.reshape(2, 2, 2, t, hd), x)
        return y

    return jax.shard_map(local, mesh=mesh, in_specs=(tok, tok, tok, wsp, wsp, wsp),
                         out_specs=tok, check_vma=False)
```

time: 421 us -> 165 us (0.39)
  matrix products: 182 us -> 0 us
  Pallas kernels: 0 us -> 162 us
  waiting for transfers between devices: 142 us -> 0 us
  local copies, waits for them, and re-layouts: 70.4 us -> 4.71 us
  starting transfers between devices: 14.7 us -> 0 us
  other arithmetic: 11.5 us -> 0 us
    dot_general x3 -> x0, matrix products: 182 us -> none  [the longest x1 63.5 us: local(): a1 = jnp.einsum('rh,ehf->erf', rx, w1, preferred_element_type=jnp.float32)]
    pallas_call x0 -> x3, Pallas kernels: none -> 162 us  [the longest x1 127 us: local(): pl.pallas_call(functools.partial(scatter_kernel, nc), out_shape=jax.Shape...]
    all_to_all x4 -> x0, waiting for transfers between devices: 142 us -> none  [the longest x1 93.3 us: local(): back = lax.all_to_all(part, axes, 0, 0, tiled=True)]
    unnamed x23 -> x3, local copies, waits for them, and re-layouts: 40.1 us -> 4.71 us
    gather x1 -> x0, local copies, waits for them, and re-layouts: 29.7 us -> none  [local(): got = back[dst, jnp.minimum(slot, cap - 1)]]
    all_to_all x4 -> x0, starting transfers between devices: 14.7 us -> none  [the longest x1 4.3 us: local(): ri = lax.all_to_all(si, axes, 0, 0, tiled=True).reshape(nd * cap, top)]
    reduce_sum x2 -> x0, other arithmetic: 7.56 us -> none  [the longest x1 6.85 us: local(): moe_out = jnp.sum(jnp.where(kept[:, :, None], got, 0.0), axis=1)]
  transfers between devices with their start and end apart: 4 -> 0, of which waited for: 2 -> 0; matrix products, arithmetic and copies ran while one was open for 8% -> 0% of each run, Pallas kernels for 0% -> 0%
where the time goes in v1:
time: 165 us; the launch traced here: 167 us
  Pallas kernels  162 us (98%)
  local copies, waits for them, and re-layouts  4.71 us (3%)
    pallas_call x1, Pallas kernels, local(): pl.pallas_call(functools.partial(scatter_kernel, nc), out_shape=jax.Shape...  127 us
    pallas_call x1, Pallas kernels, local(): pl.pallas_call(functools.partial(gather_kernel, cap), out_shape=(jax.Shap...  28.7 us
    pallas_call x1, Pallas kernels, local(): pl.pallas_call(expert_kernel, out_shape=jax.ShapeDtypeStruct((n, hd), f32...  6.28 us
    unnamed x3, local copies, waits for them, and re-layouts  4.71 us

profile of v1, /device:TPU:0, one launch (start us, length us, event | category | flops | bytes accessed | tf_op | source)
XLA Modules:
  0.0 166.7 jit_solution(6517585615798741708)
XLA Ops:
  0.0 1.4 copy.7.ids_ref
  1.4 1.4 copy.8.gates_ref
  2.8 28.7 %gather.1 = (bf16[1024,2048]{1,0:T(8,128)(2,1)}, f32[8,1024]{1,0:T(8,128)}, f32[1024,128]{1,0:T(8,128)}, s32[8,128]{1,0:T(8,128)}) custom-call(bf16[128,2048]{1,0:T(8,128)(2,1)} %x_ref.3, s32[128,6]{1,0:T(8,128)} %copy.7.ids_ref, f32[128,6]{1,0:T(8,128)} %copy.8.gates_ref), custom_call_target="tpu_custom_call" | custom-call | tf_op jit(solution)/shard_map/gather/pallas_call | solution.py:322
  31.5 6.3 %experts.1 = f32[1024,2048]{1,0:T(8,128)} custom-call(s32[8,128]{1,0:T(8,128)} %get-tuple-element.9.cum_ref, f32[8,1024]{1,0:T(8,128)} %get-tuple-element.10.pos_ref, f32[1024,128]{1,0:T(8,128)} %get-tuple-element.11.tok_ref, bf16[1024,2048]{1,0:T(8,128)(2,1)} %get-tuple-element.12.x_ref, bf16[8,2048,1408]{2,1,0:T(8,128)(2,1)} %w1_ref.1, ...), custom_call_target="tpu_custom_call" | custom-call | tf_op jit(solution)/shard_map/experts/pallas_call | solution.py:330
  37.8 127.0 %scatter.1 = bf16[128,2048]{1,0:T(8,128)(2,1)} custom-call(f32[2,2,2,128,2048]{4,3,2,1,0:T(8,128)} %bitcast.1, bf16[128,2048]{1,0:T(8,128)(2,1)} %x_ref.3), custom_call_target="tpu_custom_call" | custom-call | tf_op jit(solution)/shard_map/scatter/pallas_call | solution.py:341
  164.8 1.9 %copy.10 = bf16[128,2048]{1,0:T(8,128)(2,1)} copy(bf16[128,2048]{1,0:T(8,128)(2,1)} %scatter.1) | data formatting | bytes 1048576
